TPU v7x, 128 devices: a whole 4x4x4 slice. The times are simulated.
128 devices in a mesh: dp: 32 (over y, z, core), fsdp: 4 (over x).
Axes of the slice: x: 4, y: 4, z: 4, core: 2. Of those that a mesh axis runs over, the one named last changes fastest.
Arguments:
- tokens: bfloat16 [65536, 4096], P(('dp', 'fsdp')), may hold values from -0.75 to 0.75
- doc_ids: int32 [65536], P(('dp', 'fsdp')), may hold values from 0 to 63, never falling along the last dimension, each value on 1 to 2048 neighbouring positions
- attn_gain: float32 [4096], replicated, may hold values from 0.1 to 1.9
- mlp_gain: float32 [4096], replicated, may hold values from 0.1 to 1.9
- w_query: bfloat16 [4096, 512], P(('dp', 'fsdp')), may hold values from -1 to 1
- w_key_value: bfloat16 [4096, 256], P(('dp', 'fsdp')), may hold values from -3 to 3
- w_out: bfloat16 [512, 4096], P(None, ('dp', 'fsdp')), may hold values from -0.25 to 0.25
- w_gate: bfloat16 [4096, 1024], P(('dp', 'fsdp')), may hold values from -0.09375 to 0.09375
- w_up: bfloat16 [4096, 1024], P(('dp', 'fsdp')), may hold values from -0.09375 to 0.09375
- w_down: bfloat16 [1024, 4096], P(None, ('dp', 'fsdp')), may hold values from -0.1875 to 0.1875
Outputs:
- mixed: bfloat16 [65536, 4096], P(('dp', 'fsdp'))
Inputs may be any that keep to these rules, and one draw needn't show every extreme that they name: `doc_ids`: document numbers never fall along the pack, and every document has at most 2048 tokens.
All inputs are finite; a program needn't handle non-finite values.
Results may differ from a plain program's by a relative error of at most 0.02.
The roundings to bfloat16 on the way count: a program that leaves them out, or rounds other values in their place, can miss the bound.
Values may be sent and summed in bfloat16 or wider, within the bound.
A program may use at most 128 MiB of HBM per device.

v0:
```python
import math
import jax
import jax.numpy as jnp
from jax import lax
from jax.sharding import PartitionSpec as P

SPAN = 4
EPS = 1e-05
THETA = 500000.0
NEGATIVE = -1e30


def sent_together(arrays, axis, dim, along):
    widths = [a.shape[along] for a in arrays]
    both = jnp.concatenate(arrays, axis=along)
    out = lax.all_gather(both, axis, axis=dim, tiled=True)
    return tuple(jnp.split(out, [sum(widths[:k]) for k in range(1, len(widths))], axis=along))


def shifted(array, axis, by):
    length = lax.axis_size(axis)
    pairs = [(i, i + by) for i in range(length) if 0 <= i + by < length]
    return lax.ppermute(array, axis, pairs)


def rms_scale(values, gain):
    wide = values.astype(jnp.float32)
    power = jnp.mean(wide * wide, axis=-1, keepdims=True)
    return (wide * lax.rsqrt(power + EPS) * gain).astype(jnp.bfloat16)


def rotate(values, position):
    head = values.shape[-1]
    half = head // 2
    freqs = THETA ** (-2.0 * jnp.arange(half, dtype=jnp.float32) / head)
    angle = position.astype(jnp.float32)[:, None, None] * freqs[None, None, :]
    cosine = jnp.cos(angle)
    sine = jnp.sin(angle)
    first = values[..., :half]
    second = values[..., half:]
    return jnp.concatenate(
        [first * cosine - second * sine, second * cosine + first * sine], axis=-1
    )


def head_scores(query, keys):
    return jnp.einsum("qhd,kd->hqk", query, keys, preferred_element_type=jnp.float32) / math.sqrt(
        query.shape[-1]
    )


def weigh_values(weights, values):
    return jnp.einsum(
        "hqk,kd->qhd", weights.astype(jnp.bfloat16), values, preferred_element_type=jnp.float32
    )


def attend_live(query, halo_pairs, halo_marks, own_pairs, marks, block):
    head = query.shape[-1]
    index = jnp.arange(query.shape[0], dtype=jnp.int32)
    allowed = (marks[None, :] == marks[:, None]) & (index[None, :] <= index[:, None])
    own_scores = jnp.where(allowed[None, :, :], head_scores(query, own_pairs[:, :head]), NEGATIVE)
    count = halo_marks.shape[0] // block
    live = jnp.sum(jnp.any(halo_marks.reshape(count, block) == marks[0], axis=1).astype(jnp.int32))
    peak = jnp.max(own_scores, axis=2)
    weights = jnp.exp(own_scores - peak[:, :, None])
    totals = jnp.sum(weights, axis=2)
    mixed = weigh_values(weights, own_pairs[:, head:])

    def add_block(step, carry):
        old_peak, old_totals, old_mixed = carry
        begin = (count - 1 - step) * block
        pairs = lax.dynamic_slice_in_dim(halo_pairs, begin, block, 0)
        block_marks = lax.dynamic_slice_in_dim(halo_marks, begin, block, 0)
        same = (block_marks[None, :] == marks[:, None])[None, :, :]
        scores = jnp.where(same, head_scores(query, pairs[:, :head]), NEGATIVE)
        new_peak = jnp.maximum(old_peak, jnp.max(scores, axis=2))
        factor = jnp.exp(old_peak - new_peak)
        block_weights = jnp.exp(scores - new_peak[:, :, None])
        new_totals = old_totals * factor + jnp.sum(block_weights, axis=2)
        new_mixed = old_mixed * jnp.transpose(factor)[:, :, None] + weigh_values(
            block_weights, pairs[:, head:]
        )
        return (new_peak, new_totals, new_mixed)

    peak, totals, mixed = lax.fori_loop(0, live, add_block, (peak, totals, mixed))
    return mixed / jnp.transpose(totals)[:, :, None]


def per_device(
    tokens, doc_ids, attn_gain, mlp_gain, w_query, w_key_value, w_out, w_gate, w_up, w_down
):
    rows = tokens.shape[0]
    rank = lax.axis_index(("dp", "fsdp"))
    normed = rms_scale(tokens, attn_gain)
    query_width = w_query.shape[1]
    pair_width = w_key_value.shape[1]
    head = pair_width // 2
    heads = query_width // head
    group_query, group_pair = sent_together((w_query, w_key_value), "fsdp", 0, 1)
    pieces = sent_together((group_query, group_pair), "dp", 0, 1)
    columns = normed
    query_raw = jnp.dot(columns, pieces[0], preferred_element_type=jnp.float32)
    pair_raw = jnp.dot(columns, pieces[1], preferred_element_type=jnp.float32)
    position = rank * rows + jnp.arange(rows, dtype=jnp.int32)
    query = rotate(query_raw.reshape(rows, heads, head), position).astype(jnp.bfloat16)
    keys = rotate(pair_raw[:, None, :head], position)[:, 0, :].astype(jnp.bfloat16)
    values = pair_raw[:, head:].astype(jnp.bfloat16)
    own_pairs = jnp.concatenate([keys, values], axis=1)
    marks = doc_ids + 1
    pair_pieces = []
    mark_pieces = []
    for distance in range(SPAN, 0, -1):
        moved_pairs, moved_marks = shifted((own_pairs, marks), ("dp", "fsdp"), distance)
        pair_pieces.append(moved_pairs)
        mark_pieces.append(moved_marks)
    halo_pairs = jnp.concatenate(pair_pieces, axis=0)
    halo_marks = jnp.concatenate(mark_pieces, axis=0)
    mixed = attend_live(query, halo_pairs, halo_marks, own_pairs, marks, rows)
    attended = mixed.reshape(rows, query_width).astype(jnp.bfloat16)
    projected = jnp.dot(
        attended,
        lax.all_gather(w_out, ("dp", "fsdp"), axis=1, tiled=True),
        preferred_element_type=jnp.float32,
    )
    resid = (tokens.astype(jnp.float32) + projected).astype(jnp.bfloat16)
    resid = lax.optimization_barrier(resid)
    normed_mlp = rms_scale(resid, mlp_gain)
    group_gate, group_up = sent_together((w_gate, w_up), "fsdp", 0, 1)
    pieces = sent_together((group_gate, group_up), "dp", 0, 1)
    columns = normed_mlp
    gate = jnp.dot(columns, pieces[0], preferred_element_type=jnp.float32)
    up_value = jnp.dot(columns, pieces[1], preferred_element_type=jnp.float32)
    hidden = (jax.nn.silu(gate) * up_value).astype(jnp.bfloat16)
    down = jnp.dot(
        hidden,
        lax.all_gather(w_down, ("dp", "fsdp"), axis=1, tiled=True),
        preferred_element_type=jnp.float32,
    )
    return (resid.astype(jnp.float32) + down).astype(jnp.bfloat16)


def solution(mesh):
    in_specs = (
        P(("dp", "fsdp"), None),
        P(("dp", "fsdp")),
        P(),
        P(),
        P(("dp", "fsdp"), None),
        P(("dp", "fsdp"), None),
        P(None, ("dp", "fsdp")),
        P(("dp", "fsdp"), None),
        P(("dp", "fsdp"), None),
        P(None, ("dp", "fsdp")),
    )
    out_specs = P(("dp", "fsdp"), None)
    return jax.shard_map(
        per_device, mesh=mesh, in_specs=in_specs, out_specs=out_specs, check_vma=False
    )
```

profile of v0, /device:TPU:1, one launch (start us, length us, event | category | flops | bytes accessed | tf_op | source)
XLA Modules:
  0.0 306.7 jit_solution(3767838602492783908)
XLA Ops:
  6.5 0.8 pad_maximum_fusion.6
  7.3 11.6 %all_gather.18 = bf16[128,768]{1,0:T(8,128)(2,1)} all-gather(bf16[32,768]{1,0:T(8,128)(2,1)S(1)} %pad_maximum_fusion.6), channel_id=1, replica_groups=mesh['dp'=32,'fsdp'=4] {'fsdp'}, dimensions={0}, use_global_device_ids=true | all-gather | bytes 245760 | tf_op jit(solution)/shard_map/all_gather | solution.py:16
  18.9 0.0 all-gather.5.cloned.1.call-update
  18.9 0.0 all-gather.7.cloned.1.call-start
  19.0 0.7 all-gather.7.cloned.1.call-update
  19.7 0.0 all-gather.9.cloned.1.call-start
  19.7 0.9 pad_maximum_fusion.4
  20.6 10.6 %all_gather.21 = bf16[128,2048]{1,0:T(8,128)(2,1)} all-gather(bf16[32,2048]{1,0:T(8,128)(2,1)S(1)} %pad_maximum_fusion.4), channel_id=1, replica_groups=mesh['dp'=32,'fsdp'=4] {'fsdp'}, dimensions={0}, use_global_device_ids=true | all-gather | bytes 655360 | tf_op jit(solution)/shard_map/all_gather | solution.py:16
  31.2 0.0 all-gather.9.cloned.1.call-update
  31.3 0.0 all-gather.11.cloned.1.call-start
  31.3 0.7 broadcast_add_fusion
  32.0 9.7 %collective-permute-start = (s32[512]{0:T(512)S(1)}, s32[512]{0:T(512)S(1)}, u32[]{:S(2)}, u32[]{:S(2)}) collective-permute-start(s32[512]{0:T(512)S(1)} %broadcast_add_fusion), channel_id=1, source_target_pairs={{0,4},{1,5},{2,6},{3,7},{4,8},{5,9},{6,10},{7,11},{8,12},{9,13},{1... | collective-permute-start | bytes 6152 | tf_op jit(solution)/shard_map/ppermute | solution.py:23
  41.7 3.9 %collective-permute-start.1 = (s32[512]{0:T(512)S(1)}, s32[512]{0:T(512)S(1)}, u32[]{:S(2)}, u32[]{:S(2)}) collective-permute-start(s32[512]{0:T(512)S(1)} %broadcast_add_fusion), channel_id=1, source_target_pairs={{0,3},{1,4},{2,5},{3,6},{4,7},{5,8},{6,9},{7,10},{8,11},{9,12},{10... | collective-permute-start | bytes 6152 | tf_op jit(solution)/shard_map/ppermute | solution.py:23
  45.6 2.2 collective-permute-start.2
  47.8 2.2 collective-permute-start.3
  50.0 0.0 all-gather.11.cloned.1.call-update
  50.1 0.2 fusion.48
  50.3 3.1 %fusion.17 = f32[512]{0:T(512)S(1)} fusion(bf16[512,4096]{1,0:T(8,128)(2,1)} %param.12), kind=kLoop, calls=%fused_computation.25 | loop fusion | flops 6290944 | bytes 4196352 | tf_op jit(solution)/shard_map/reduce_sum | solution.py:28
  53.4 1.0 multiply_cosine_fusion
  54.4 0.5 slice.36
  55.0 0.7 broadcast_compare_fusion.1
  55.7 0.1 reduce_or.9
  55.8 0.7 convert_reduce_fusion
  56.5 16.5 %all-gather.5.cloned.1.call-done = bf16[4096,768]{1,0:T(8,128)(2,1)} async-done(((bf16[128,768]{1,0:T(8,128)(2,1)}), bf16[4096,768]{1,0:T(8,128)(2,1)}) %all-gather.5.cloned.1.call-update) | async-done | bytes 6291472 | tf_op jit(solution)/shard_map/all_gather | solution.py:16
  73.0 4.6 %fusion.34 = f32[512,256]{0,1:T(8,128)S(1)} fusion(bf16[4096,768]{1,0:T(8,128)(2,1)} %all-gather.5.cloned.1.call-done, bf16[512,4096]{1,0:T(8,128)(2,1)} %param.12, f32[4096]{0:T(1024)S(1)} %copy-done.8, f32[512]{0:T(512)S(1)} %add_rsqrt_fusion.1), kind=kOutput, calls=%fused_computation.44 | convolution fusion | flops 1082130432 | bytes 6834176 | tf_op jit(solution)/shard_map/dot_general | solution.py:104
  77.6 0.0 copy-start.4
  77.7 0.6 fusion.54
  78.2 0.7 pad_maximum_fusion.2
  79.0 2.3 collective-permute-start.4
  81.3 4.3 %collective-permute-start.5 = (bf16[512,256]{0,1:T(8,128)(2,1)}, bf16[512,256]{0,1:T(8,128)(2,1)}, u32[]{:S(2)}, u32[]{:S(2)}) collective-permute-start(bf16[512,256]{0,1:T(8,128)(2,1)} %pad_maximum_fusion.2), channel_id=1, source_target_pairs={{0,3},{1,4},{2,5},{3,6},{4,7},{5,8},{6,9},{7,10},{8,11},{9,12},{10... | collective-permute-start | bytes 786440 | tf_op jit(solution)/shard_map/ppermute | solution.py:23
  85.6 2.4 collective-permute-start.6
  88.0 2.6 collective-permute-start.7
  90.7 2.6 fusion.29
  93.3 0.1 fusion.64
  93.4 0.3 copy.32
  93.7 0.3 copy.33
  94.1 0.3 subtract_convert_fusion
  94.3 0.0 copy-start.5
  94.4 0.3 pad_maximum_fusion.1
  94.7 0.9 fusion.33
  95.6 1.3 fusion.41
  97.0 0.9 fusion.32
  97.9 0.1 collective-permute-done.6
  98.0 5.3 %collective-permute-done.7 = bf16[512,256]{0,1:T(8,128)(2,1)} collective-permute-done((bf16[512,256]{0,1:T(8,128)(2,1)}, bf16[512,256]{0,1:T(8,128)(2,1)}, u32[]{:S(2)}, u32[]{:S(2)}) %collective-permute-start.7) | collective-permute-done | bytes 262176 | tf_op jit(solution)/shard_map/ppermute | solution.py:23
  103.4 1.3 pad_maximum_fusion
  104.7 9.5 %while.14 = (s32[]{:T(128)}, f32[4,512]{1,0:T(4,128)S(1)}, f32[4,512]{1,0:T(4,128)S(1)}, f32[512,4,128]{0,2,1:T(8,128)S(1)}, s32[]{:T(128)}, /*index=5*/s32[2048...) while((s32[]{:T(128)}, f32[4,512]{1,0:T(4,128)S(1)}, ...), condition=%wide.region_8.9_spmd, body=%wide.region_5.8_spmd.sunk | while | flops 549197824 | bytes 33431808 | solution.py:86
  105.3 0.1 dynamic_slice.7
  105.4 0.2 broadcast_compare_fusion.3
  105.6 2.9 fusion.80
  108.5 0.0 copy-start
  108.5 3.8 %fusion.83 = f32[512,4,128]{0,2,1:T(8,128)S(1)} fusion(f32[512,512,4]{1,0,2:T(8,128)} %get-tuple-element.168, f32[4,512]{1,0:T(4,128)S(1)} %get-tuple-element.201, pred[512,512]{0,1:T(8,128)(4,1)S(1)} %broadcast_compare_fusion.3, f32[512,4,128]{0,2,1:T(8,128)S(1)} %get-tuple-element.188, f32[512,4]{0,1:T(4,128)S(1)} %get-tuple-element.169, ...), kind=kOutput, calls=%fused_computation.8.clone.1 | convolution fusion | flops 273154048 | bytes 6701064 | tf_op jit(solution)/shard_map/while/body/hqk,kd->qhd/dot_general | solution.py:53
  112.4 0.9 fusion.82
  114.2 0.1 divide_convert_fusion
  114.3 30.9 %all-gather.7.cloned.1.call-done = bf16[512,4096]{0,1:T(8,128)(2,1)} async-done(((bf16[512,32]{0,1:T(8,128)(2,1)}), bf16[512,4096]{0,1:T(8,128)(2,1)}) %all-gather.7.cloned.1.call-update) | async-done | bytes 4194320 | tf_op jit(solution)/shard_map/all_gather | solution.py:123
  145.2 5.9 %fusion.20 = bf16[512,4096]{1,0:T(8,128)(2,1)S(1)} fusion(bf16[512,4096]{1,0:T(8,128)(2,1)} %param.12, bf16[512,512]{0,1:T(8,128)(2,1)S(1)} %bitcast.82, bf16[512,4096]{0,1:T(8,128)(2,1)} %all-gather.7.cloned.1.call-done), kind=kOutput, calls=%fused_computation.28 | convolution fusion | flops 2153775104 | bytes 13107200 | tf_op jit(solution)/shard_map/dot_general | solution.py:121
  151.1 0.0 copy-start.2
  151.1 2.0 copy-done.2
  153.1 0.9 fusion.21
  154.0 63.8 %all-gather.9.cloned.1.call-done = bf16[4096,2048]{1,0:T(8,128)(2,1)} async-done(((bf16[128,2048]{1,0:T(8,128)(2,1)}), bf16[4096,2048]{1,0:T(8,128)(2,1)}) %all-gather.9.cloned.1.call-update) | async-done | bytes 16777232 | tf_op jit(solution)/shard_map/all_gather | solution.py:16
  217.8 8.4 %fusion.27 = f32[512,1024]{1,0:T(8,128)S(1)} fusion(bf16[4096,2048]{1,0:T(8,128)(2,1)} %all-gather.9.cloned.1.call-done, bf16[512,4096]{1,0:T(8,128)(2,1)} %copy-done.2, f32[4096]{0:T(1024)S(1)} %copy-done.9, f32[512]{0:T(512)S(1)} %add_rsqrt_fusion), kind=kOutput, calls=%fused_computation.35 | convolution fusion | flops 4303355904 | bytes 14698496 | tf_op jit(solution)/shard_map/dot_general | solution.py:132
  226.3 2.3 copy-done.6
  228.6 4.7 %multiply_convert_fusion = bf16[512,1024]{1,0:T(8,128)(2,1)S(1)} fusion(f32[512,1024]{1,0:T(8,128)S(1)} %fusion.27, bf16[4096,2048]{1,0:T(8,128)(2,1)S(1)} %copy-done.6, bf16[512,4096]{1,0:T(8,128)(2,1)S(1)} %copy-done.3, f32[4096]{0:T(1024)S(1)} %copy-done.9, f32[512]{0:T(512)S(1)} %add_rsqrt_fusion), kind=kOutput, calls=%fused_computation.46 | convolution fusion | flops 4306501632 | bytes 15747072 | tf_op jit(solution)/shard_map/dot_general | solution.py:133
  233.3 56.6 %all-gather.11.cloned.1.call-done = bf16[1024,4096]{0,1:T(8,128)(2,1)} async-done(((bf16[1024,32]{0,1:T(8,128)(2,1)}), bf16[1024,4096]{0,1:T(8,128)(2,1)}) %all-gather.11.cloned.1.call-update) | async-done | bytes 8388624 | tf_op jit(solution)/shard_map/all_gather | solution.py:137
  289.9 10.2 %fusion.24 = bf16[512,4096]{1,0:T(8,128)(2,1)} fusion(bf16[512,4096]{1,0:T(8,128)(2,1)} %copy-done.2, bf16[512,1024]{1,0:T(8,128)(2,1)S(1)} %multiply_convert_fusion, bf16[1024,4096]{0,1:T(8,128)(2,1)} %all-gather.11.cloned.1.call-done), kind=kOutput, calls=%fused_computation.32 | convolution fusion | flops 4301258752 | bytes 17825792 | tf_op jit(solution)/shard_map/dot_general | solution.py:135
  (37 shorter events, 0.2 us)
Async XLA Ops:
  6.5 66.5 %copy-start.8 = (f32[4096]{0:T(1024)S(1)}, f32[4096]{0:T(1024)}, u32[]{:S(2)}) copy-start(f32[4096]{0:T(1024)} %param.14) | copy-start | bytes 49156
  6.5 66.5 %all-gather.5.cloned.1.call-start = ((), (), s32[]{:S(2)}) async-start(), calls=%async_computation | async-start | bytes 6488064 | tf_op jit(solution)/shard_map/all_gather | solution.py:16
  18.9 126.3 %all-gather.7.cloned.1.call-start = ((), (), s32[]{:S(2)}) async-start(), calls=%async_computation.1 | async-start | bytes 4227072 | tf_op jit(solution)/shard_map/all_gather | solution.py:123
  19.7 198.2 %all-gather.9.cloned.1.call-start = ((), (), s32[]{:S(2)}) async-start(), calls=%async_computation.2 | async-start | bytes 17301504 | tf_op jit(solution)/shard_map/all_gather | solution.py:16
  31.3 258.7 %all-gather.11.cloned.1.call-start = ((), (), s32[]{:S(2)}) async-start(), calls=%async_computation.3 | async-start | bytes 8454144 | tf_op jit(solution)/shard_map/all_gather | solution.py:137
  32.0 22.9 %collective-permute-start = (s32[512]{0:T(512)S(1)}, s32[512]{0:T(512)S(1)}, u32[]{:S(2)}, u32[]{:S(2)}) collective-permute-start(s32[512]{0:T(512)S(1)} %broadcast_add_fusion), channel_id=1, source_target_pairs={{0,4},{1,5},{2,6},{3,7},{4,8},{5,9},{6,10},{7,11},{8,12},{9,13},{1... | collective-permute-start | bytes 6152 | tf_op jit(solution)/shard_map/ppermute | solution.py:23
  41.7 13.2 %collective-permute-start.1 = (s32[512]{0:T(512)S(1)}, s32[512]{0:T(512)S(1)}, u32[]{:S(2)}, u32[]{:S(2)}) collective-permute-start(s32[512]{0:T(512)S(1)} %broadcast_add_fusion), channel_id=1, source_target_pairs={{0,3},{1,4},{2,5},{3,6},{4,7},{5,8},{6,9},{7,10},{8,11},{9,12},{10... | collective-permute-start | bytes 6152 | tf_op jit(solution)/shard_map/ppermute | solution.py:23
  45.6 9.3 %collective-permute-start.2 = (s32[512]{0:T(512)S(1)}, s32[512]{0:T(512)S(1)}, u32[]{:S(2)}, u32[]{:S(2)}) collective-permute-start(s32[512]{0:T(512)S(1)} %broadcast_add_fusion), channel_id=1, source_target_pairs={{0,2},{1,3},{2,4},{3,5},{4,6},{5,7},{6,8},{7,9},{8,10},{9,11},{10,... | collective-permute-start | bytes 6152 | tf_op jit(solution)/shard_map/ppermute | solution.py:23
  47.8 7.1 %collective-permute-start.3 = (s32[512]{0:T(512)S(1)}, s32[512]{0:T(512)S(1)}, u32[]{:S(2)}, u32[]{:S(2)}) collective-permute-start(s32[512]{0:T(512)S(1)} %broadcast_add_fusion), channel_id=1, source_target_pairs={{0,1},{1,2},{2,3},{3,4},{4,5},{5,6},{6,7},{7,8},{8,9},{9,10},{10,1... | collective-permute-start | bytes 6152 | tf_op jit(solution)/shard_map/ppermute | solution.py:23
  73.0 17.6 %copy-start.1 = (bf16[512,4096]{1,0:T(8,128)(2,1)S(1)}, bf16[512,4096]{1,0:T(8,128)(2,1)}, u32[]{:S(2)}) copy-start(bf16[512,4096]{1,0:T(8,128)(2,1)} %param.12) | copy-start | bytes 12582916
  73.0 17.7 %copy-start.7 = (bf16[4096,768]{1,0:T(8,128)(2,1)S(1)}, bf16[4096,768]{1,0:T(8,128)(2,1)}, u32[]{:S(2)}) copy-start(bf16[4096,768]{1,0:T(8,128)(2,1)} %all-gather.5.cloned.1.call-done) | copy-start | bytes 18874372
  77.6 10.4 %copy-start.4 = (f32[512,256]{0,1:T(8,128)}, f32[512,256]{0,1:T(8,128)S(1)}, u32[]{:S(2)}) copy-start(f32[512,256]{0,1:T(8,128)S(1)} %fusion.34) | copy-start | bytes 1572868
  79.0 18.9 %collective-permute-start.4 = (bf16[512,256]{0,1:T(8,128)(2,1)}, bf16[512,256]{0,1:T(8,128)(2,1)}, u32[]{:S(2)}, u32[]{:S(2)}) collective-permute-start(bf16[512,256]{0,1:T(8,128)(2,1)} %pad_maximum_fusion.2), channel_id=1, source_target_pairs={{0,4},{1,5},{2,6},{3,7},{4,8},{5,9},{6,10},{7,11},{8,12},{9,13},{1... | collective-permute-start | bytes 786440 | tf_op jit(solution)/shard_map/ppermute | solution.py:23
  81.3 16.6 %collective-permute-start.5 = (bf16[512,256]{0,1:T(8,128)(2,1)}, bf16[512,256]{0,1:T(8,128)(2,1)}, u32[]{:S(2)}, u32[]{:S(2)}) collective-permute-start(bf16[512,256]{0,1:T(8,128)(2,1)} %pad_maximum_fusion.2), channel_id=1, source_target_pairs={{0,3},{1,4},{2,5},{3,6},{4,7},{5,8},{6,9},{7,10},{8,11},{9,12},{10... | collective-permute-start | bytes 786440 | tf_op jit(solution)/shard_map/ppermute | solution.py:23
  85.6 12.5 %collective-permute-start.6 = (bf16[512,256]{0,1:T(8,128)(2,1)}, bf16[512,256]{0,1:T(8,128)(2,1)}, u32[]{:S(2)}, u32[]{:S(2)}) collective-permute-start(bf16[512,256]{0,1:T(8,128)(2,1)} %pad_maximum_fusion.2), channel_id=1, source_target_pairs={{0,2},{1,3},{2,4},{3,5},{4,6},{5,7},{6,8},{7,9},{8,10},{9,11},{10,... | collective-permute-start | bytes 786440 | tf_op jit(solution)/shard_map/ppermute | solution.py:23
  88.0 15.4 %collective-permute-start.7 = (bf16[512,256]{0,1:T(8,128)(2,1)}, bf16[512,256]{0,1:T(8,128)(2,1)}, u32[]{:S(2)}, u32[]{:S(2)}) collective-permute-start(bf16[512,256]{0,1:T(8,128)(2,1)} %pad_maximum_fusion.2), channel_id=1, source_target_pairs={{0,1},{1,2},{2,3},{3,4},{4,5},{5,6},{6,7},{7,8},{8,9},{9,10},{10,1... | collective-permute-start | bytes 786440 | tf_op jit(solution)/shard_map/ppermute | solution.py:23
  94.3 1.3 copy-start.5
  108.5 3.8 %copy-start = (f32[512,512,4]{1,0,2:T(8,128)S(1)}, f32[512,512,4]{1,0,2:T(8,128)}, u32[]{:S(2)}) copy-start(f32[512,512,4]{1,0,2:T(8,128)} %get-tuple-element.168) | copy-start | bytes 12582916 | tf_op jit(solution)/shard_map/while
  151.1 2.0 copy-start.2
  153.1 64.7 %copy-start.9 = (f32[4096]{0:T(1024)S(1)}, f32[4096]{0:T(1024)}, u32[]{:S(2)}) copy-start(f32[4096]{0:T(1024)} %param.15) | copy-start | bytes 49156
  217.8 8.4 %copy-start.3 = (bf16[512,4096]{1,0:T(8,128)(2,1)S(1)}, bf16[512,4096]{1,0:T(8,128)(2,1)}, u32[]{:S(2)}) copy-start(bf16[512,4096]{1,0:T(8,128)(2,1)} %copy-done.2) | copy-start | bytes 12582916
  217.8 10.7 %copy-start.6 = (bf16[4096,2048]{1,0:T(8,128)(2,1)S(1)}, bf16[4096,2048]{1,0:T(8,128)(2,1)}, u32[]{:S(2)}) copy-start(bf16[4096,2048]{1,0:T(8,128)(2,1)} %all-gather.9.cloned.1.call-done) | copy-start | bytes 50331652
Sparse Core Ops, SparseCore 0:
  19.0 53.9 all-gather.4
  76.2 69.0 all-gather.6
  147.5 70.2 all-gather.8
  220.8 69.0 all-gather.10
where the time goes:
time: 307 us
  waiting for transfers between devices  174 us (57%)
  matrix products  45.4 us (15%)
  starting transfers between devices  29.8 us (10%)
  blocking collectives  22.2 us (7%)
  other arithmetic  14.4 us (5%)
  between operations  13.5 us (4%)
  local copies, waits for them, and re-layouts  5.78 us (2%)
    all_gather x2, waiting for transfers between devices, sent_together(): out = lax.all_gather(both, axis, axis=dim, tiled=True)  80.3 us
    all_gather x1, waiting for transfers between devices, per_device(): lax.all_gather(w_down, ('dp', 'fsdp'), axis=1, tiled=True)  56.6 us
    all_gather x1, waiting for transfers between devices, per_device(): lax.all_gather(w_out, ('dp', 'fsdp'), axis=1, tiled=True)  30.9 us
    ppermute x8, starting transfers between devices, shifted(): return lax.ppermute(array, axis, pairs)  29.7 us
    all_gather x2, blocking collectives, sent_together(): out = lax.all_gather(both, axis, axis=dim, tiled=True)  22.2 us
    dot_general x1, matrix products, per_device(): jnp.dot(hidden, lax.all_gather(w_down, ('dp', 'fsdp'), axis=1, tiled=True...  10.2 us
    dot_general x1, matrix products, per_device(): gate = jnp.dot(columns, pieces[0], preferred_element_type=jnp.float32)  8.4 us
  transfers between devices with their start and end apart: 12, of which 6 were waited for; matrix products, arithmetic and copies ran while one was open for 16% of the time, Pallas kernels for 0%

commit v1 on v0

--- a/solution.py
+++ b/solution.py
@@ -118,11 +118,13 @@
     halo_marks = jnp.concatenate(mark_pieces, axis=0)
     mixed = attend_live(query, halo_pairs, halo_marks, own_pairs, marks, rows)
     attended = mixed.reshape(rows, query_width).astype(jnp.bfloat16)
-    projected = jnp.dot(
-        attended,
-        lax.all_gather(w_out, ("dp", "fsdp"), axis=1, tiled=True),
-        preferred_element_type=jnp.float32,
+    points_press = lambda w_in: jnp.concatenate(
+        lax.all_to_all(
+            jnp.stack(lax.axis_size(("dp", "fsdp")) * [w_in], axis=0), ("dp", "fsdp"), 0, 0
+        ),
+        axis=1,
     )
+    projected = jnp.dot(attended, points_press(w_out), preferred_element_type=jnp.float32)
     resid = (tokens.astype(jnp.float32) + projected).astype(jnp.bfloat16)
     resid = lax.optimization_barrier(resid)
     normed_mlp = rms_scale(resid, mlp_gain)

time: 307 us -> 283 us (0.922)
  waiting for transfers between devices: 174 us -> 137 us
  starting transfers between devices: 29.8 us -> 39.3 us
  local copies, waits for them, and re-layouts: 5.78 us -> 9.06 us
    all_gather x1 -> x0, waiting for transfers between devices: 30.9 us -> none  [per_device(): lax.all_gather(w_out, ('dp', 'fsdp'), axis=1, tiled=True)]
    all_to_all x0 -> x1, starting transfers between devices: none -> 10.4 us  [per_device(): lax.all_to_all(jnp.stack(lax.axis_size(('dp', 'fsdp')) * [w_in], axis=0),...]
    all_gather x2, waiting for transfers between devices: 80.3 us -> 74.3 us  [sent_together(): out = lax.all_gather(both, axis, axis=dim, tiled=True)]
    another operation x0 -> x1, local copies, waits for them, and re-layouts: none -> 3.3 us  [per_device(): jnp.stack(lax.axis_size(('dp', 'fsdp')) * [w_in], axis=0)]
  transfers between devices with their start and end apart: 12 -> 12, of which waited for: 6 -> 5; matrix products, arithmetic and copies ran while one was open for 16% -> 19% of each run, Pallas kernels for 0% -> 0%
where the time goes in v1:
time: 283 us; the launch traced here: 282 us
  waiting for transfers between devices  137 us (48%)
  matrix products  45.4 us (16%)
  starting transfers between devices  39.3 us (14%)
  blocking collectives  22.2 us (8%)
  other arithmetic  14.4 us (5%)
  between operations  13.5 us (5%)
  local copies, waits for them, and re-layouts  9.06 us (3%)
    all_gather x2, waiting for transfers between devices, sent_together(): out = lax.all_gather(both, axis, axis=dim, tiled=True)  74.3 us
    all_gather x1, waiting for transfers between devices, per_device(): lax.all_gather(w_down, ('dp', 'fsdp'), axis=1, tiled=True)  56.8 us
    ppermute x8, starting transfers between devices, shifted(): return lax.ppermute(array, axis, pairs)  28.8 us
    all_gather x2, blocking collectives, sent_together(): out = lax.all_gather(both, axis, axis=dim, tiled=True)  22.2 us
    all_to_all x1, starting transfers between devices, per_device(): lax.all_to_all(jnp.stack(lax.axis_size(('dp', 'fsdp')) * [w_in], axis=0),...  10.4 us
    dot_general x1, matrix products, per_device(): jnp.dot(hidden, lax.all_gather(w_down, ('dp', 'fsdp'), axis=1, tiled=True...  10.2 us
    dot_general x1, matrix products, per_device(): gate = jnp.dot(columns, pieces[0], preferred_element_type=jnp.float32)  8.41 us
    dot_general x1, matrix products, per_device(): jnp.dot(attended, points_press(w_out), preferred_element_type=jnp.float32)  5.87 us
  transfers between devices with their start and end apart: 12, of which 5 were waited for; matrix products, arithmetic and copies ran while one was open for 19% of the time, Pallas kernels for 0%

profile of v1, /device:TPU:1, one launch (start us, length us, event | category | flops | bytes accessed | tf_op | source)
XLA Modules:
  0.0 282.2 jit_solution(9416689780375060481)
XLA Ops:
  6.5 0.8 pad_maximum_fusion.6
  7.3 11.6 %all_gather.15 = bf16[128,768]{1,0:T(8,128)(2,1)} all-gather(bf16[32,768]{1,0:T(8,128)(2,1)S(1)} %pad_maximum_fusion.6), channel_id=1, replica_groups=mesh['dp'=32,'fsdp'=4] {'fsdp'}, dimensions={0}, use_global_device_ids=true | all-gather | bytes 245760 | tf_op jit(solution)/shard_map/all_gather | solution.py:16
  18.9 0.0 all-gather.4.cloned.1.call-update
  18.9 0.0 all-gather.6.cloned.1.call-start
  19.0 0.9 pad_maximum_fusion.4
  19.8 10.6 %all_gather.17 = bf16[128,2048]{1,0:T(8,128)(2,1)} all-gather(bf16[32,2048]{1,0:T(8,128)(2,1)S(1)} %pad_maximum_fusion.4), channel_id=1, replica_groups=mesh['dp'=32,'fsdp'=4] {'fsdp'}, dimensions={0}, use_global_device_ids=true | all-gather | bytes 655360 | tf_op jit(solution)/shard_map/all_gather | solution.py:16
  30.5 0.0 all-gather.6.cloned.1.call-update
  30.5 0.7 broadcast_add_fusion
  31.2 9.7 %collective-permute-start = (s32[512]{0:T(512)S(1)}, s32[512]{0:T(512)S(1)}, u32[]{:S(2)}, u32[]{:S(2)}) collective-permute-start(s32[512]{0:T(512)S(1)} %broadcast_add_fusion), channel_id=1, source_target_pairs={{0,4},{1,5},{2,6},{3,7},{4,8},{5,9},{6,10},{7,11},{8,12},{9,13},{1... | collective-permute-start | bytes 6152 | tf_op jit(solution)/shard_map/ppermute | solution.py:23
  40.9 3.9 %collective-permute-start.1 = (s32[512]{0:T(512)S(1)}, s32[512]{0:T(512)S(1)}, u32[]{:S(2)}, u32[]{:S(2)}) collective-permute-start(s32[512]{0:T(512)S(1)} %broadcast_add_fusion), channel_id=1, source_target_pairs={{0,3},{1,4},{2,5},{3,6},{4,7},{5,8},{6,9},{7,10},{8,11},{9,12},{10... | collective-permute-start | bytes 6152 | tf_op jit(solution)/shard_map/ppermute | solution.py:23
  44.8 2.2 collective-permute-start.2
  47.0 2.2 collective-permute-start.3
  49.2 3.3 %stack.2 = bf16[128,512,32]{1,2,0:T(8,128)(2,1)} broadcast(bf16[512,32]{0,1:T(8,128)(2,1)} %param.18), dimensions={1,2} | broadcast | bytes 4227072 | tf_op jit(solution)/shard_map/stack | solution.py:123
  52.5 10.4 %all-to-all-start = ((bf16[128,512,32]{1,2,0:T(8,128)(2,1)}), bf16[128,512,32]{1,2,0:T(8,128)(2,1)}, u32[]{:S(2)}, u32[]{:S(2)}) async-start(bf16[128,512,32]{1,2,0:T(8,128)(2,1)} %stack.2), calls=%async_computation | async-start | bytes 8388608 | tf_op jit(solution)/shard_map/all_to_all | solution.py:122
  62.9 0.0 copy-start.8
  63.0 0.0 all-gather.8.cloned.1.call-start
  63.0 0.7 all-gather.8.cloned.1.call-update
  63.7 0.2 fusion.48
  63.9 3.2 %fusion.17 = f32[512]{0:T(512)S(1)} fusion(bf16[512,4096]{1,0:T(8,128)(2,1)} %param.12), kind=kLoop, calls=%fused_computation.25 | loop fusion | flops 6290944 | bytes 4196352 | tf_op jit(solution)/shard_map/reduce_sum | solution.py:28
  67.2 1.0 multiply_cosine_fusion
  68.2 0.5 slice.36
  68.7 0.0 collective-permute-done
  68.7 0.0 collective-permute-done.1
  68.7 0.0 collective-permute-done.2
  68.7 0.6 broadcast_compare_fusion.1
  69.3 0.1 reduce_or.9
  69.5 0.7 convert_reduce_fusion
  70.2 46.5 %all-gather.4.cloned.1.call-done = bf16[4096,768]{1,0:T(8,128)(2,1)} async-done(((bf16[128,768]{1,0:T(8,128)(2,1)}), bf16[4096,768]{1,0:T(8,128)(2,1)}) %all-gather.4.cloned.1.call-update) | async-done | bytes 6291472 | tf_op jit(solution)/shard_map/all_gather | solution.py:16
  116.7 4.6 %fusion.34 = f32[512,256]{0,1:T(8,128)S(1)} fusion(bf16[4096,768]{1,0:T(8,128)(2,1)} %all-gather.4.cloned.1.call-done, bf16[512,4096]{1,0:T(8,128)(2,1)} %param.12, f32[4096]{0:T(1024)S(1)} %copy-done.8, f32[512]{0:T(512)S(1)} %add_rsqrt_fusion.1), kind=kOutput, calls=%fused_computation.44 | convolution fusion | flops 1082130432 | bytes 6834176 | tf_op jit(solution)/shard_map/dot_general | solution.py:104
  121.3 0.6 fusion.54
  121.9 0.7 pad_maximum_fusion.2
  122.6 1.9 collective-permute-start.4
  124.5 4.3 %collective-permute-start.5 = (bf16[512,256]{0,1:T(8,128)(2,1)}, bf16[512,256]{0,1:T(8,128)(2,1)}, u32[]{:S(2)}, u32[]{:S(2)}) collective-permute-start(bf16[512,256]{0,1:T(8,128)(2,1)} %pad_maximum_fusion.2), channel_id=1, source_target_pairs={{0,3},{1,4},{2,5},{3,6},{4,7},{5,8},{6,9},{7,10},{8,11},{9,12},{10... | collective-permute-start | bytes 786440 | tf_op jit(solution)/shard_map/ppermute | solution.py:23
  128.9 2.2 collective-permute-start.6
  131.1 2.4 collective-permute-start.7
  133.5 2.6 fusion.29
  136.1 0.1 fusion.64
  136.2 0.3 copy.40
  136.5 0.3 copy.41
  136.9 0.3 subtract_convert_fusion
  137.2 0.3 pad_maximum_fusion.1
  137.5 0.9 fusion.33
  138.4 1.3 fusion.41
  139.8 0.9 fusion.32
  140.7 0.4 collective-permute-done.6
  141.2 4.4 %collective-permute-done.7 = bf16[512,256]{0,1:T(8,128)(2,1)} collective-permute-done((bf16[512,256]{0,1:T(8,128)(2,1)}, bf16[512,256]{0,1:T(8,128)(2,1)}, u32[]{:S(2)}, u32[]{:S(2)}) %collective-permute-start.7) | collective-permute-done | bytes 262176 | tf_op jit(solution)/shard_map/ppermute | solution.py:23
  145.6 1.3 pad_maximum_fusion
  146.9 9.6 %while.14 = (s32[]{:T(128)}, f32[4,512]{1,0:T(4,128)S(1)}, f32[4,512]{1,0:T(4,128)S(1)}, f32[512,4,128]{0,2,1:T(8,128)S(1)}, s32[]{:T(128)}, /*index=5*/s32[2048...) while((s32[]{:T(128)}, f32[4,512]{1,0:T(4,128)S(1)}, ...), condition=%wide.region_8.9_spmd, body=%wide.region_5.8_spmd.sunk | while | flops 549197824 | bytes 33431808 | solution.py:86
  147.6 0.1 dynamic_slice.7
  147.7 0.2 broadcast_compare_fusion.3
  147.9 2.9 %fusion.80 = (f32[4,512]{1,0:T(4,128)S(1)}, f32[512,512,4]{1,0,2:T(8,128)}) fusion(pred[512,512]{0,1:T(8,128)(4,1)S(1)} %broadcast_compare_fusion.3, bf16[512,4,128]{2,0,1:T(8,128)(2,1)S(1)} %get-tuple-element.217, bf16[2048,256]{0,1:T(8,128)(2,1)S(1)} %get-tuple-element.216, s32[]{:T(128)S(6)} %select_n.42), kind=kOutput, calls=%fused_computation.4.clone.1 | convolution fusion | flops 271579136 | bytes 5120004 | tf_op jit(solution)/shard_map/while/body/qhd,kd->hqk/dot_general | solution.py:47
  150.8 3.8 %fusion.83 = f32[512,4,128]{0,2,1:T(8,128)S(1)} fusion(f32[512,512,4]{1,0,2:T(8,128)} %get-tuple-element.177, f32[4,512]{1,0:T(4,128)S(1)} %get-tuple-element.210, pred[512,512]{0,1:T(8,128)(4,1)S(1)} %broadcast_compare_fusion.3, f32[512,4,128]{0,2,1:T(8,128)S(1)} %get-tuple-element.197, f32[512,4]{0,1:T(4,128)S(1)} %get-tuple-element.178, ...), kind=kOutput, calls=%fused_computation.8.clone.1 | convolution fusion | flops 273154048 | bytes 6701064 | tf_op jit(solution)/shard_map/while/body/hqk,kd->qhd/dot_general | solution.py:53
  154.6 0.9 fusion.82
  156.5 0.1 divide_convert_fusion
  156.6 5.9 %fusion.20 = bf16[512,4096]{1,0:T(8,128)(2,1)S(1)} fusion(bf16[512,4096]{1,0:T(8,128)(2,1)} %param.12, bf16[512,512]{0,1:T(8,128)(2,1)S(1)} %bitcast.85, bf16[512,4096]{0,1:T(8,128)(2,1)} %bitcast.16), kind=kOutput, calls=%fused_computation.28 | convolution fusion | flops 2153775104 | bytes 13107200 | tf_op jit(solution)/shard_map/dot_general | solution.py:127
  162.5 0.0 copy-start.2
  162.5 2.0 copy-done.2
  164.5 0.9 fusion.21
  165.4 27.8 %all-gather.6.cloned.1.call-done = bf16[4096,2048]{1,0:T(8,128)(2,1)} async-done(((bf16[128,2048]{1,0:T(8,128)(2,1)}), bf16[4096,2048]{1,0:T(8,128)(2,1)}) %all-gather.6.cloned.1.call-update) | async-done | bytes 16777232 | tf_op jit(solution)/shard_map/all_gather | solution.py:16
  193.2 8.4 %fusion.27 = f32[512,1024]{1,0:T(8,128)S(1)} fusion(bf16[4096,2048]{1,0:T(8,128)(2,1)} %all-gather.6.cloned.1.call-done, bf16[512,4096]{1,0:T(8,128)(2,1)} %copy-done.2, f32[4096]{0:T(1024)S(1)} %copy-done.9, f32[512]{0:T(512)S(1)} %add_rsqrt_fusion), kind=kOutput, calls=%fused_computation.35 | convolution fusion | flops 4303355904 | bytes 14698496 | tf_op jit(solution)/shard_map/dot_general | solution.py:134
  201.7 2.3 copy-done.6
  203.9 4.7 %multiply_convert_fusion = bf16[512,1024]{1,0:T(8,128)(2,1)S(1)} fusion(f32[512,1024]{1,0:T(8,128)S(1)} %fusion.27, bf16[4096,2048]{1,0:T(8,128)(2,1)S(1)} %copy-done.6, bf16[512,4096]{1,0:T(8,128)(2,1)S(1)} %copy-done.3, f32[4096]{0:T(1024)S(1)} %copy-done.9, f32[512]{0:T(512)S(1)} %add_rsqrt_fusion), kind=kOutput, calls=%fused_computation.46 | convolution fusion | flops 4306501632 | bytes 15747072 | tf_op jit(solution)/shard_map/dot_general | solution.py:135
  208.7 56.8 %all-gather.8.cloned.1.call-done = bf16[1024,4096]{0,1:T(8,128)(2,1)} async-done(((bf16[1024,32]{0,1:T(8,128)(2,1)}), bf16[1024,4096]{0,1:T(8,128)(2,1)}) %all-gather.8.cloned.1.call-update) | async-done | bytes 8388624 | tf_op jit(solution)/shard_map/all_gather | solution.py:139
  265.5 10.2 %fusion.24 = bf16[512,4096]{1,0:T(8,128)(2,1)} fusion(bf16[512,4096]{1,0:T(8,128)(2,1)} %copy-done.2, bf16[512,1024]{1,0:T(8,128)(2,1)S(1)} %multiply_convert_fusion, bf16[1024,4096]{0,1:T(8,128)(2,1)} %all-gather.8.cloned.1.call-done), kind=kOutput, calls=%fused_computation.32 | convolution fusion | flops 4301258752 | bytes 17825792 | tf_op jit(solution)/shard_map/dot_general | solution.py:137
  (37 shorter events, 0.2 us)
Async XLA Ops:
  6.5 110.1 %all-gather.4.cloned.1.call-start = ((), (), s32[]{:S(2)}) async-start(), calls=%async_computation.1 | async-start | bytes 6488064 | tf_op jit(solution)/shard_map/all_gather | solution.py:16
  18.9 174.3 %all-gather.6.cloned.1.call-start = ((), (), s32[]{:S(2)}) async-start(), calls=%async_computation.2 | async-start | bytes 17301504 | tf_op jit(solution)/shard_map/all_gather | solution.py:16
  31.2 37.5 %collective-permute-start = (s32[512]{0:T(512)S(1)}, s32[512]{0:T(512)S(1)}, u32[]{:S(2)}, u32[]{:S(2)}) collective-permute-start(s32[512]{0:T(512)S(1)} %broadcast_add_fusion), channel_id=1, source_target_pairs={{0,4},{1,5},{2,6},{3,7},{4,8},{5,9},{6,10},{7,11},{8,12},{9,13},{1... | collective-permute-start | bytes 6152 | tf_op jit(solution)/shard_map/ppermute | solution.py:23
  40.9 27.8 %collective-permute-start.1 = (s32[512]{0:T(512)S(1)}, s32[512]{0:T(512)S(1)}, u32[]{:S(2)}, u32[]{:S(2)}) collective-permute-start(s32[512]{0:T(512)S(1)} %broadcast_add_fusion), channel_id=1, source_target_pairs={{0,3},{1,4},{2,5},{3,6},{4,7},{5,8},{6,9},{7,10},{8,11},{9,12},{10... | collective-permute-start | bytes 6152 | tf_op jit(solution)/shard_map/ppermute | solution.py:23
  44.8 23.9 %collective-permute-start.2 = (s32[512]{0:T(512)S(1)}, s32[512]{0:T(512)S(1)}, u32[]{:S(2)}, u32[]{:S(2)}) collective-permute-start(s32[512]{0:T(512)S(1)} %broadcast_add_fusion), channel_id=1, source_target_pairs={{0,2},{1,3},{2,4},{3,5},{4,6},{5,7},{6,8},{7,9},{8,10},{9,11},{10,... | collective-permute-start | bytes 6152 | tf_op jit(solution)/shard_map/ppermute | solution.py:23
  47.0 21.7 %collective-permute-start.3 = (s32[512]{0:T(512)S(1)}, s32[512]{0:T(512)S(1)}, u32[]{:S(2)}, u32[]{:S(2)}) collective-permute-start(s32[512]{0:T(512)S(1)} %broadcast_add_fusion), channel_id=1, source_target_pairs={{0,1},{1,2},{2,3},{3,4},{4,5},{5,6},{6,7},{7,8},{8,9},{9,10},{10,1... | collective-permute-start | bytes 6152 | tf_op jit(solution)/shard_map/ppermute | solution.py:23
  52.5 104.1 %all-to-all-start = ((bf16[128,512,32]{1,2,0:T(8,128)(2,1)}), bf16[128,512,32]{1,2,0:T(8,128)(2,1)}, u32[]{:S(2)}, u32[]{:S(2)}) async-start(bf16[128,512,32]{1,2,0:T(8,128)(2,1)} %stack.2), calls=%async_computation | async-start | bytes 8388608 | tf_op jit(solution)/shard_map/all_to_all | solution.py:122
  62.9 53.7 %copy-start.8 = (f32[4096]{0:T(1024)S(1)}, f32[4096]{0:T(1024)}, u32[]{:S(2)}) copy-start(f32[4096]{0:T(1024)} %param.14) | copy-start | bytes 49156
  63.0 202.5 %all-gather.8.cloned.1.call-start = ((), (), s32[]{:S(2)}) async-start(), calls=%async_computation.3 | async-start | bytes 8454144 | tf_op jit(solution)/shard_map/all_gather | solution.py:139
  116.7 16.8 %copy-start.1 = (bf16[512,4096]{1,0:T(8,128)(2,1)S(1)}, bf16[512,4096]{1,0:T(8,128)(2,1)}, u32[]{:S(2)}) copy-start(bf16[512,4096]{1,0:T(8,128)(2,1)} %param.12) | copy-start | bytes 12582916
  116.7 16.8 %copy-start.7 = (bf16[4096,768]{1,0:T(8,128)(2,1)S(1)}, bf16[4096,768]{1,0:T(8,128)(2,1)}, u32[]{:S(2)}) copy-start(bf16[4096,768]{1,0:T(8,128)(2,1)} %all-gather.4.cloned.1.call-done) | copy-start | bytes 18874372
  121.3 9.8 %copy-start.4 = (f32[512,256]{0,1:T(8,128)}, f32[512,256]{0,1:T(8,128)S(1)}, u32[]{:S(2)}) copy-start(f32[512,256]{0,1:T(8,128)S(1)} %fusion.34) | copy-start | bytes 1572868
  122.6 18.1 %collective-permute-start.4 = (bf16[512,256]{0,1:T(8,128)(2,1)}, bf16[512,256]{0,1:T(8,128)(2,1)}, u32[]{:S(2)}, u32[]{:S(2)}) collective-permute-start(bf16[512,256]{0,1:T(8,128)(2,1)} %pad_maximum_fusion.2), channel_id=1, source_target_pairs={{0,4},{1,5},{2,6},{3,7},{4,8},{5,9},{6,10},{7,11},{8,12},{9,13},{1... | collective-permute-start | bytes 786440 | tf_op jit(solution)/shard_map/ppermute | solution.py:23
  124.5 16.2 %collective-permute-start.5 = (bf16[512,256]{0,1:T(8,128)(2,1)}, bf16[512,256]{0,1:T(8,128)(2,1)}, u32[]{:S(2)}, u32[]{:S(2)}) collective-permute-start(bf16[512,256]{0,1:T(8,128)(2,1)} %pad_maximum_fusion.2), channel_id=1, source_target_pairs={{0,3},{1,4},{2,5},{3,6},{4,7},{5,8},{6,9},{7,10},{8,11},{9,12},{10... | collective-permute-start | bytes 786440 | tf_op jit(solution)/shard_map/ppermute | solution.py:23
  128.9 12.3 %collective-permute-start.6 = (bf16[512,256]{0,1:T(8,128)(2,1)}, bf16[512,256]{0,1:T(8,128)(2,1)}, u32[]{:S(2)}, u32[]{:S(2)}) collective-permute-start(bf16[512,256]{0,1:T(8,128)(2,1)} %pad_maximum_fusion.2), channel_id=1, source_target_pairs={{0,2},{1,3},{2,4},{3,5},{4,6},{5,7},{6,8},{7,9},{8,10},{9,11},{10,... | collective-permute-start | bytes 786440 | tf_op jit(solution)/shard_map/ppermute | solution.py:23
  131.1 14.5 %collective-permute-start.7 = (bf16[512,256]{0,1:T(8,128)(2,1)}, bf16[512,256]{0,1:T(8,128)(2,1)}, u32[]{:S(2)}, u32[]{:S(2)}) collective-permute-start(bf16[512,256]{0,1:T(8,128)(2,1)} %pad_maximum_fusion.2), channel_id=1, source_target_pairs={{0,1},{1,2},{2,3},{3,4},{4,5},{5,6},{6,7},{7,8},{8,9},{9,10},{10,1... | collective-permute-start | bytes 786440 | tf_op jit(solution)/shard_map/ppermute | solution.py:23
  137.2 1.3 copy-start.5
  150.8 3.8 %copy-start = (f32[512,512,4]{1,0,2:T(8,128)S(1)}, f32[512,512,4]{1,0,2:T(8,128)}, u32[]{:S(2)}) copy-start(f32[512,512,4]{1,0,2:T(8,128)} %get-tuple-element.177) | copy-start | bytes 12582916 | tf_op jit(solution)/shard_map/while
  162.5 2.0 copy-start.2
  164.5 28.7 %copy-start.9 = (f32[4096]{0:T(1024)S(1)}, f32[4096]{0:T(1024)}, u32[]{:S(2)}) copy-start(f32[4096]{0:T(1024)} %param.15) | copy-start | bytes 49156
  193.2 8.4 %copy-start.3 = (bf16[512,4096]{1,0:T(8,128)(2,1)S(1)}, bf16[512,4096]{1,0:T(8,128)(2,1)}, u32[]{:S(2)}) copy-start(bf16[512,4096]{1,0:T(8,128)(2,1)} %copy-done.2) | copy-start | bytes 12582916
  193.2 10.7 %copy-start.6 = (bf16[4096,2048]{1,0:T(8,128)(2,1)S(1)}, bf16[4096,2048]{1,0:T(8,128)(2,1)}, u32[]{:S(2)}) copy-start(bf16[4096,2048]{1,0:T(8,128)(2,1)} %all-gather.6.cloned.1.call-done) | copy-start | bytes 50331652
Sparse Core Ops, SparseCore 0:
  19.0 97.5 all-gather.3
  118.9 74.2 all-gather.5
  196.4 69.0 all-gather.7
